TPU v7x, 32 devices: a whole 2x2x4 slice. The times are simulated.
32 devices in a mesh: blk: 8 (over z, x), dp: 4 (over y, core).
Axes of the slice: x: 2, y: 2, z: 4, core: 2. Of those that a mesh axis runs over, the one named last changes fastest.
Arguments:
- tokens: bfloat16 [4096, 3072], P(('blk', 'dp')), may hold values from -6 to 6
- expert_ids: int32 [4096, 2], P(('blk', 'dp')), may hold values from 0 to 7, as said below
- gate_num: int32 [4096], P(('blk', 'dp')), may hold values from 1 to 255
- gate_weight: bfloat16 [3072, 8192], P('dp', 'blk'), may hold values from -0.109375 to 0.109375
- up_weight: bfloat16 [3072, 8192], P('dp', 'blk'), may hold values from -0.109375 to 0.109375
- down_weight: bfloat16 [8192, 3072], P(('blk', 'dp')), may hold values from -0.0625 to 0.0625
Outputs:
- moe_out: bfloat16 [4096, 3072], P(('blk', 'dp'))
Inputs may be any that keep to these rules, and one draw needn't show every extreme that they name: `expert_ids`: each row names two different experts. Among the 128 rows of one device (aligned blocks), between 1 and 64 name expert 0, and in every draw the rows of some device include exactly 64 such rows.
All inputs are finite; a program needn't handle non-finite values.
Results may differ from a plain program's by a relative error of at most 0.018.
Values may be sent and summed in bfloat16 or wider, within the bound.
A program may use at most 192 MiB of HBM per device.

v0:
```python
import jax
import jax.numpy as jnp
from jax import lax
from jax.sharding import PartitionSpec as P

GATE_SCALE = 256.0


def route_table(expert_ids, slot_count):
    hits = jnp.sum((expert_ids == 0).astype(jnp.int32), axis=1)
    position = jnp.cumsum(hits) - 1
    marks = (hits[:, None] > 0) & (
        position[:, None] == jnp.arange(slot_count, dtype=jnp.int32)[None, :]
    )
    return marks.astype(jnp.float32)


def gate_values(expert_ids, gate_num):
    first = gate_num.astype(jnp.float32) / GATE_SCALE
    return jnp.where(expert_ids[:, 0] == 0, first, 0.0) + jnp.where(
        expert_ids[:, 1] == 0, 1.0 - first, 0.0
    )


def on_device(tokens, expert_ids, gate_num, gate_weight, up_weight, down_weight):
    slot_count = tokens.shape[0] // 2
    marks = route_table(expert_ids, slot_count)
    packed = lax.dot_general(
        marks.astype(jnp.bfloat16),
        tokens,
        (((0,), (0,)), ((), ())),
        preferred_element_type=jnp.float32,
    ).astype(jnp.bfloat16)
    down_local = lax.all_gather(down_weight, "dp", axis=0, tiled=True)
    gathered = lax.all_gather(packed, "blk", axis=0, tiled=True)

    def add_rows(piece):
        return jnp.dot(gathered, piece, preferred_element_type=jnp.float32)

    gate = add_rows(lax.all_gather(gate_weight, "dp", axis=0, tiled=True))
    up = add_rows(lax.all_gather(up_weight, "dp", axis=0, tiled=True))
    hidden = (jax.nn.silu(gate) * up).astype(jnp.bfloat16)
    term = jnp.dot(hidden, down_local, preferred_element_type=jnp.float32).astype(jnp.bfloat16)
    term = lax.optimization_barrier(term)
    own_rows = lax.psum_scatter(
        term.astype(jnp.float32).astype(jnp.bfloat16), "blk", scatter_dimension=0, tiled=True
    ).astype(jnp.float32)
    expanded = jnp.dot(marks, own_rows, precision=lax.Precision.HIGHEST)
    weights = gate_values(expert_ids, gate_num)
    return (weights[:, None] * expanded).astype(jnp.bfloat16)


def solution(mesh):
    return jax.shard_map(
        on_device,
        mesh=mesh,
        in_specs=(
            P(("blk", "dp"), None),
            P(("blk", "dp"), None),
            P(("blk", "dp")),
            P("dp", "blk"),
            P("dp", "blk"),
            P(("blk", "dp"), None),
        ),
        out_specs=P(("blk", "dp"), None),
        check_vma=False,
    )
```

profile of v0, /device:TPU:0, one launch (start us, length us, event | category | flops | bytes accessed | tf_op | source)
XLA Modules:
  0.0 311.9 jit_solution(8863363476095033535)
XLA Ops:
  6.5 0.0 copy-start
  6.5 0.0 all-gather.5.cloned.1.call-start
  6.5 0.8 fusion.7
  7.3 0.1 copy.8
  7.4 0.2 reduce-window.8
  7.6 0.1 add_reduce_fusion
  7.7 0.0 copy-done
  7.7 1.1 convolution_convert_fusion.1
  8.9 0.0 all-gather.5.cloned.1.call-update
  8.9 0.0 all-gather.7.cloned.1.call-start
  8.9 0.7 all-gather.7.cloned.1.call-update
  9.6 0.0 all-gather.11.cloned.1.call-start
  9.7 0.7 all-gather.11.cloned.1.call-update
  10.4 0.0 all-gather.9.cloned.1.call-start
  10.4 0.5 all-gather.9.cloned.1.call-update
  10.9 0.0 reduce-scatter.2.cloned.1.call-start
  11.0 61.3 %all-gather.5.cloned.1.call-done = bf16[512,3072]{1,0:T(8,128)(2,1)} async-done(((bf16[64,3072]{1,0:T(8,128)(2,1)}), bf16[512,3072]{1,0:T(8,128)(2,1)}) %all-gather.5.cloned.1.call-update) | async-done | bytes 3145744 | tf_op jit(solution)/shard_map/all_gather | solution.py:35
  72.3 46.6 %all-gather.7.cloned.1.call-done = bf16[3072,1024]{1,0:T(8,128)(2,1)} async-done(((bf16[768,1024]{1,0:T(8,128)(2,1)}), bf16[3072,1024]{1,0:T(8,128)(2,1)}) %all-gather.7.cloned.1.call-update) | async-done | bytes 6291472 | tf_op jit(solution)/shard_map/all_gather | solution.py:40
  118.9 6.4 %fusion.10 = f32[512,1024]{1,0:T(8,128)S(1)} fusion(bf16[512,3072]{1,0:T(8,128)(2,1)} %all-gather.5.cloned.1.call-done, bf16[3072,1024]{1,0:T(8,128)(2,1)} %all-gather.7.cloned.1.call-done), kind=kOutput, calls=%fused_computation.20 | convolution fusion | flops 3221225472 | bytes 11534336 | tf_op jit(solution)/shard_map/dot_general | solution.py:38
  125.4 41.5 %all-gather.11.cloned.1.call-done = bf16[1024,3072]{1,0:T(8,128)(2,1)} async-done(((bf16[256,3072]{1,0:T(8,128)(2,1)}), bf16[1024,3072]{1,0:T(8,128)(2,1)}) %all-gather.11.cloned.1.call-update) | async-done | bytes 6291472 | tf_op jit(solution)/shard_map/all_gather | solution.py:34
  166.9 47.8 %all-gather.9.cloned.1.call-done = bf16[3072,1024]{1,0:T(8,128)(2,1)} async-done(((bf16[768,1024]{1,0:T(8,128)(2,1)}), bf16[3072,1024]{1,0:T(8,128)(2,1)}) %all-gather.9.cloned.1.call-update) | async-done | bytes 6291472 | tf_op jit(solution)/shard_map/all_gather | solution.py:41
  214.7 14.0 %convolution_convert_fusion = bf16[512,3072]{1,0:T(8,128)(2,1)} fusion(bf16[1024,3072]{1,0:T(8,128)(2,1)} %all-gather.11.cloned.1.call-done, f32[512,1024]{1,0:T(8,128)S(1)} %fusion.10, bf16[512,3072]{1,0:T(8,128)(2,1)} %all-gather.5.cloned.1.call-done, bf16[3072,1024]{1,0:T(8,128)(2,1)} %all-gather.9.cloned.1.call-done), kind=kOutput, calls=%fused_computation | convolution fusion | flops 6447169536 | bytes 20971520 | tf_op jit(solution)/shard_map/dot_general | solution.py:43
  228.6 0.0 copy-start.1
  228.6 0.0 copy-start.2
  228.6 0.0 reduce-scatter.2.cloned.1.call-update
  228.7 0.7 copy-done.1
  229.3 0.0 copy-done.2
  229.3 73.7 %reduce-scatter.2.cloned.1.call-done = bf16[64,3072]{1,0:T(8,128)(2,1)} async-done(((bf16[512,3072]{1,0:T(8,128)(2,1)}), bf16[64,3072]{1,0:T(8,128)(2,1)}) %reduce-scatter.2.cloned.1.call-update) | async-done | bytes 393232 | tf_op jit(solution)/shard_map/reduce_scatter | solution.py:45
  303.1 2.3 fusion
  (2 shorter events, 0.0 us)
Async XLA Ops:
  6.5 1.2 copy-start
  6.5 65.7 %all-gather.5.cloned.1.call-start = ((), (), s32[]{:S(2)}) async-start(), calls=%async_computation.1 | async-start | bytes 3538944 | tf_op jit(solution)/shard_map/all_gather | solution.py:35
  8.9 110.0 %all-gather.7.cloned.1.call-start = ((), (), s32[]{:S(2)}) async-start(), calls=%async_computation.2 | async-start | bytes 7864320 | tf_op jit(solution)/shard_map/all_gather | solution.py:40
  9.6 157.2 %all-gather.11.cloned.1.call-start = ((), (), s32[]{:S(2)}) async-start(), calls=%async_computation.4 | async-start | bytes 7864320 | tf_op jit(solution)/shard_map/all_gather | solution.py:34
  10.4 204.3 %all-gather.9.cloned.1.call-start = ((), (), s32[]{:S(2)}) async-start(), calls=%async_computation.3 | async-start | bytes 7864320 | tf_op jit(solution)/shard_map/all_gather | solution.py:41
  10.9 292.1 %reduce-scatter.2.cloned.1.call-start = ((), (), s32[]{:S(2)}) async-start(), calls=%async_computation.5 | async-start | bytes 3538944 | tf_op jit(solution)/shard_map/reduce_scatter | solution.py:45
  228.6 0.7 copy-start.1
  228.6 0.7 copy-start.2
Sparse Core Ops, SparseCore 0:
  9.5 62.7 all-gather.4
  73.8 45.0 all-gather.6
  120.5 46.3 all-gather.10
  168.3 46.3 all-gather.8
  228.8 74.2 reduce-scatter.1
where the time goes:
time: 312 us
  waiting for transfers between devices  273 us (88%)
  matrix products  23.8 us (8%)
  between operations  13.2 us (4%)
    reduce_scatter x1, waiting for transfers between devices, on_device(): lax.psum_scatter(term.astype(jnp.float32).astype(jnp.bfloat16), 'blk', sc...  73.7 us
    all_gather x1, waiting for transfers between devices, on_device(): gathered = lax.all_gather(packed, 'blk', axis=0, tiled=True)  61.3 us
    all_gather x1, waiting for transfers between devices, on_device(): up = add_rows(lax.all_gather(up_weight, 'dp', axis=0, tiled=True))  47.8 us
    all_gather x1, waiting for transfers between devices, on_device(): gate = add_rows(lax.all_gather(gate_weight, 'dp', axis=0, tiled=True))  46.6 us
    all_gather x1, waiting for transfers between devices, on_device(): down_local = lax.all_gather(down_weight, 'dp', axis=0, tiled=True)  41.5 us
    dot_general x1, matrix products, on_device(): jnp.dot(hidden, down_local, preferred_element_type=jnp.float32)  14 us
    dot_general x1, matrix products, add_rows(): return jnp.dot(gathered, piece, preferred_element_type=jnp.float32)  6.44 us
  transfers between devices with their start and end apart: 5, of which 5 were waited for; matrix products, arithmetic and copies ran while one was open for 2% of the time, Pallas kernels for 0%

commit v1 on v0

v1 whole, which is shorter than its diff:
```python
import functools

import jax
import jax.numpy as jnp
from jax import lax
from jax.experimental import pallas as pl
from jax.experimental.pallas import tpu as pltpu
from jax.sharding import PartitionSpec as P

GATE_SCALE = 256.0
MESH = pl.DeviceIdType.MESH
F32 = jnp.float32
BF16 = jnp.bfloat16


def largest_tile(size, most):
    tile = most
    while size % tile:
        tile //= 2
    return tile


def kernel(nb, nd, rows_ch, cols_ch,
           tokens, ids, num, gate_w, up_w, down_w,
           slots_out, marks_out,
           x, gw, uw, dw, accg, accu, hidden, term, got1, part, got2,
           loc_sem, own_send, own_recv, y_send, y_recv, fwd_send, fwd_recv,
           z_send, z_recv, x_send, x_recv, p1_send, p1_recv, p2_send, p2_recv):
    k = lax.axis_index("blk")
    j = lax.axis_index("dp")
    na, nc = nb // 2, nd // 2
    a, b = k // 2, k % 2
    y, core = j // 2, j % 2
    t_dev, depth = tokens.shape
    slots = t_dev // 2
    gate_rows, ff = gate_w.shape
    down_rows = down_w.shape[0]
    n_ch = gate_rows // rows_ch
    nq = depth // cols_ch
    mate = (k, y * 2 + 1 - core)
    x_peer = (a * 2 + 1 - b, j)

    def y_chip(d):
        return lax.rem(y + d, nc)

    def z_chip(d):
        return lax.rem(a + d, na)

    def y_dev(d):
        return (k, y_chip(d) * 2 + core)

    def z_dev(d):
        return (z_chip(d) * 2 + b, j)

    def remote(src, dst, send, recv, device):
        return pltpu.make_async_remote_copy(
            src_ref=src, dst_ref=dst, send_sem=send, recv_sem=recv,
            device_id=device, device_id_type=MESH)

    def piece(p, shard):
        if p < 2 * n_ch:
            rows = pl.ds((p // 2) * rows_ch, rows_ch)
            src, dst = ((gate_w, gw), (up_w, uw))[p % 2]
            return src.at[rows, :], dst.at[shard, rows, :]
        q = p - 2 * n_ch
        return down_w.at[:, pl.ds(q * cols_ch, cols_ch)], dw.at[q, shard]

    pieces = 2 * n_ch + nq

    peers = [mate, x_peer] + [y_dev(d) for d in range(1, nc)] + [z_dev(d) for d in range(1, na)]
    barrier = pltpu.get_barrier_semaphore()
    for peer in peers:
        pl.semaphore_signal(barrier, inc=1, device_id=peer, device_id_type=MESH)
    local = []
    for p in range(pieces):
        src, dst = piece(p, j)
        local.append(pltpu.make_async_copy(src, dst, loc_sem.at[p]))
        local[-1].start()
    pl.semaphore_wait(barrier, len(peers))

    y_copies = []
    for p in range(pieces):
        src, dst = piece(p, j)
        for d in range(1, nc):
            y_copies.append(remote(src, dst, y_send.at[d - 1, p], y_recv.at[d - 1, p], y_dev(d)))
            y_copies[-1].start()

    hit0 = (ids[:, 0:1] == 0).astype(F32)
    hit1 = (ids[:, 1:2] == 0).astype(F32)
    hit = hit0 + hit1
    row = lax.broadcasted_iota(jnp.int32, (t_dev, t_dev), 0)
    col = lax.broadcasted_iota(jnp.int32, (t_dev, t_dev), 1)
    lower = (col <= row).astype(F32)
    place = jnp.dot(lower.astype(BF16), jnp.broadcast_to(hit, (t_dev, t_dev)).astype(BF16),
                    preferred_element_type=F32) - 1.0
    marks = jnp.where(place == col.astype(F32), 1.0, 0.0) * hit
    marks_out[...] = marks[:, :slots].astype(BF16)
    m0 = (marks * hit0).T[:slots]
    m1 = (marks * hit1).T[:slots]
    first = num[...].astype(F32) / GATE_SCALE
    weight = jnp.sum(m0 * first + m1 * (1.0 - first), axis=1, keepdims=True)
    packer = (m0 + m1).astype(BF16)

    def block(aa, bb):
        return pl.ds(pl.multiple_of((bb * na + aa) * slots, slots), slots)

    mine = block(a, b)
    for s in range(nd):
        columns = tokens[:, s * gate_rows:(s + 1) * gate_rows]
        x[s, mine, :] = jnp.dot(packer, columns, preferred_element_type=F32).astype(BF16)

    t_copies = []
    for d in range(1, na):
        t_copies.append(remote(x.at[:, mine, :], x.at[:, mine, :], z_send.at[d - 1], z_recv.at[d - 1], z_dev(d)))
        t_copies[-1].start()
    t_copies.append(remote(x.at[:, mine, :], x.at[:, mine, :], x_send.at[0], x_recv.at[0], x_peer))
    t_copies[-1].start()

    own_copies = []
    for p in range(pieces):
        src, dst = piece(p, j)
        own_copies.append(remote(src, dst, own_send.at[p], own_recv.at[p], mate))
        own_copies[-1].start()

    accg[...] = jnp.zeros_like(accg)
    accu[...] = jnp.zeros_like(accu)

    for d in range(1, na):
        came = block(lax.rem(a + na - d, na), b)
        remote(x.at[:, came, :], x.at[:, came, :], z_send.at[d - 1], z_recv.at[d - 1], z_dev(d)).wait_recv()
        t_copies.append(remote(x.at[:, came, :], x.at[:, came, :], x_send.at[d], x_recv.at[d], x_peer))
        t_copies[-1].start()
    for d in range(na):
        came = block(lax.rem(a + na - d, na), 1 - b)
        remote(x.at[:, came, :], x.at[:, came, :], x_send.at[d], x_recv.at[d], x_peer).wait_recv()

    tile = largest_tile(ff, 256)

    def add_rows(shard, c):
        r0 = c * rows_ch

        @pl.loop(0, ff // tile)
        def _(n):
            cols = pl.ds(pl.multiple_of(n * tile, tile), tile)
            left = x[shard, :, pl.ds(r0, rows_ch)]
            accg[:, cols] += jnp.dot(left, gw[shard, pl.ds(r0, rows_ch), cols], preferred_element_type=F32)
            accu[:, cols] += jnp.dot(left, uw[shard, pl.ds(r0, rows_ch), cols], preferred_element_type=F32)

    other = y * 2 + 1 - core
    for c in range(n_ch):
        local[2 * c].wait()
        local[2 * c + 1].wait()
        add_rows(j, c)
    for c in range(n_ch):
        for p in (2 * c, 2 * c + 1):
            own_copies[p].wait_recv()
        add_rows(other, c)

    fwd_copies = []

    def forward(p):
        for d in range(1, nc):
            came = lax.rem(y + nc - d, nc) * 2 + core
            src, dst = piece(p, came)
            remote(src, dst, y_send.at[d - 1, p], y_recv.at[d - 1, p], y_dev(d)).wait_recv()
            fwd_copies.append(remote(dst, dst, fwd_send.at[d - 1, p], fwd_recv.at[d - 1, p], mate))
            fwd_copies[-1].start()

    def take(p):
        for d in range(1, nc):
            came = lax.rem(y + nc - d, nc) * 2 + 1 - core
            src, dst = piece(p, came)
            remote(dst, dst, fwd_send.at[d - 1, p], fwd_recv.at[d - 1, p], mate).wait_recv()

    for c in range(n_ch):
        forward(2 * c)
        forward(2 * c + 1)
        for d in range(1, nc):
            add_rows(lax.rem(y + nc - d, nc) * 2 + core, c)
        take(2 * c)
        take(2 * c + 1)
        for d in range(1, nc):
            add_rows(lax.rem(y + nc - d, nc) * 2 + 1 - core, c)

    rows_all = nb * slots
    htile = largest_tile(rows_all, 64)

    @pl.loop(0, rows_all // htile)
    def _(i):
        rows = pl.ds(pl.multiple_of(i * htile, htile), htile)
        g = accg[rows, :]
        hidden[rows, :] = (g / (1.0 + jnp.exp(-g)) * accu[rows, :]).astype(BF16)

    half = na * slots
    mtile = largest_tile(rows_all, 256)
    sums = []

    def multiply(q):
        p = 2 * n_ch + q
        forward(p)
        local[p].wait()
        own_copies[p].wait_recv()
        take(p)

        @pl.loop(0, rows_all // mtile)
        def _(i):
            rows = pl.ds(pl.multiple_of(i * mtile, mtile), mtile)
            term[q, rows, :] = jnp.dot(
                hidden[rows, :], dw[q].reshape(nd * down_rows, cols_ch),
                preferred_element_type=F32).astype(BF16)

        away = pl.ds(pl.multiple_of((1 - b) * half, half), half)
        sums.append(remote(term.at[q, away, :], got1.at[q], p1_send.at[q], p1_recv.at[q], x_peer))
        sums[-1].start()

    def pair(q):
        remote(got1.at[q], got1.at[q], p1_send.at[q], p1_recv.at[q], x_peer).wait_recv()
        here = pl.ds(pl.multiple_of(b * half, half), half)
        part[q] = (term[q, here, :].astype(F32) + got1[q].astype(F32)).astype(BF16)
        for d in range(1, na):
            rows = pl.ds(pl.multiple_of(z_chip(d) * slots, slots), slots)
            sums.append(remote(part.at[q, rows, :], got2.at[q, d - 1],
                               p2_send.at[q, d - 1], p2_recv.at[q, d - 1], z_dev(d)))
            sums[-1].start()

    def finish(q):
        for d in range(1, na):
            remote(got2.at[q, d - 1], got2.at[q, d - 1],
                   p2_send.at[q, d - 1], p2_recv.at[q, d - 1], z_dev(d)).wait_recv()
        total = part[q, pl.ds(pl.multiple_of(a * slots, slots), slots), :].astype(F32)
        for d in range(1, na):
            total += got2[q, d - 1].astype(F32)
        slots_out[:, pl.ds(q * cols_ch, cols_ch)] = (weight * total).astype(BF16)

    for q in range(nq + 2):
        if q < nq:
            multiply(q)
        if 1 <= q <= nq:
            pair(q - 1)
        if q >= 2:
            finish(q - 2)

    for copy in y_copies + t_copies + own_copies + fwd_copies + sums:
        copy.wait_send()


def on_device(nb, nd, tokens, expert_ids, gate_num, gate_weight, up_weight, down_weight):
    t_dev, depth = tokens.shape
    slots = t_dev // 2
    gate_rows, ff = gate_weight.shape
    down_rows = down_weight.shape[0]
    rows_ch = largest_tile(gate_rows, 256)
    if rows_ch % 128:
        rows_ch = gate_rows
    cols_ch = largest_tile(depth, 512)
    n_ch, nq = gate_rows // rows_ch, depth // cols_ch
    pieces = 2 * n_ch + nq
    na, nc = nb // 2, nd // 2
    rows_all = nb * slots
    dma = pltpu.SemaphoreType.DMA
    vmem = pl.BlockSpec(memory_space=pltpu.VMEM)
    hbm = pl.BlockSpec(memory_space=pl.ANY)
    far, deep = max(nc - 1, 1), max(na - 1, 1)
    packed, marks = pl.pallas_call(
        functools.partial(kernel, nb, nd, rows_ch, cols_ch),
        out_shape=(jax.ShapeDtypeStruct((slots, depth), BF16),
                   jax.ShapeDtypeStruct((t_dev, slots), BF16)),
        in_specs=[vmem, vmem, vmem, hbm, hbm, hbm],
        out_specs=(vmem, vmem),
        scratch_shapes=[
            pltpu.VMEM((nd, rows_all, gate_rows), BF16),
            pltpu.VMEM((nd, gate_rows, ff), BF16),
            pltpu.VMEM((nd, gate_rows, ff), BF16),
            pltpu.VMEM((nq, nd, down_rows, cols_ch), BF16),
            pltpu.VMEM((rows_all, ff), F32),
            pltpu.VMEM((rows_all, ff), F32),
            pltpu.VMEM((rows_all, ff), BF16),
            pltpu.VMEM((nq, rows_all, cols_ch), BF16),
            pltpu.VMEM((nq, na * slots, cols_ch), BF16),
            pltpu.VMEM((nq, na * slots, cols_ch), BF16),
            pltpu.VMEM((nq, deep, slots, cols_ch), BF16),
            dma((pieces,)), dma((pieces,)), dma((pieces,)),
            dma((far, pieces)), dma((far, pieces)), dma((far, pieces)), dma((far, pieces)),
            dma((deep,)), dma((deep,)), dma((na,)), dma((na,)),
            dma((nq,)), dma((nq,)), dma((nq, deep)), dma((nq, deep)),
        ],
        compiler_params=pltpu.CompilerParams(
            collective_id=0, has_side_effects=True, vmem_limit_bytes=60 * 1024 * 1024),
    )(tokens, expert_ids, gate_num.reshape(1, t_dev), gate_weight, up_weight, down_weight)
    return jnp.dot(marks, packed, preferred_element_type=F32).astype(BF16)


def solution(mesh):
    return jax.shard_map(
        functools.partial(on_device, mesh.shape["blk"], mesh.shape["dp"]),
        mesh=mesh,
        in_specs=(
            P(("blk", "dp"), None),
            P(("blk", "dp"), None),
            P(("blk", "dp")),
            P("dp", "blk"),
            P("dp", "blk"),
            P(("blk", "dp"), None),
        ),
        out_specs=P(("blk", "dp"), None),
        check_vma=False,
    )
```

time: 312 us -> 132 us (0.42)
  waiting for transfers between devices: 273 us -> 0 us
  Pallas kernels: 0 us -> 128 us
  matrix products: 23.8 us -> 2.25 us
  between operations: 13.2 us -> 0.01 us
    all_gather x4 -> x0, waiting for transfers between devices: 197 us -> none  [the longest x1 61.3 us: on_device(): gathered = lax.all_gather(packed, 'blk', axis=0, tiled=True)]
    pallas_call x0 -> x1, Pallas kernels: none -> 128 us  [on_device(): pl.pallas_call(functools.partial(kernel, nb, nd, rows_ch, cols_ch), out_s...]
    reduce_scatter x1 -> x0, waiting for transfers between devices: 73.7 us -> none  [on_device(): lax.psum_scatter(term.astype(jnp.float32).astype(jnp.bfloat16), 'blk', sc...]
    dot_general x4 -> x1, matrix products: 23.8 us -> 2.25 us  [on_device(): return jnp.dot(marks, packed, preferred_element_type=F32).astype(BF16)]
  transfers between devices with their start and end apart: 5 -> 0, of which waited for: 5 -> 0; matrix products, arithmetic and copies ran while one was open for 2% -> 0% of each run, Pallas kernels for 0% -> 0%
where the time goes in v1:
time: 132 us
  Pallas kernels  128 us (97%)
  matrix products  2.25 us (2%)
  local copies, waits for them, and re-layouts  1.41 us (1%)
    pallas_call x1, Pallas kernels, on_device(): pl.pallas_call(functools.partial(kernel, nb, nd, rows_ch, cols_ch), out_s...  128 us

profile of v1, /device:TPU:0, one launch (start us, length us, event | category | flops | bytes accessed | tf_op | source)
XLA Modules:
  0.0 131.6 jit_solution(1540529737426875866)
XLA Ops:
  0.0 1.4 %copy.7.ids = s32[128,2]{1,0:T(8,128)} copy(s32[128,2]{0,1:T(2,128)} %param.7) | data formatting | bytes 2048 | tf_op args[1]
  1.4 128.0 %shard_map.64 = (bf16[64,3072]{1,0:T(8,128)(2,1)}, bf16[128,64]{1,0:T(8,128)(2,1)}) custom-call(bf16[128,3072]{1,0:T(8,128)(2,1)} %tokens.1, s32[128,2]{1,0:T(8,128)} %copy.7.ids, s32[1,128]{1,0:T(1,128)} %bitcast.3, bf16[768,1024]{1,0:T(8,128)(2,1)} %gate_w.1, bf16[768,1024]{1,0:T(8,128)(2,1)} %up_w.1, bf16[256,3072]{1,0:T(8,128)(2,1)} %down_w.1), custom_call_target="tpu_custom_call" | custom-call | tf_op jit(solution)/shard_map/pallas_call | solution.py:264
  129.4 2.2 %convolution_convert_fusion = bf16[128,3072]{1,0:T(8,128)(2,1)} fusion(bf16[128,64]{1,0:T(8,128)(2,1)} %get-tuple-element.7, bf16[64,3072]{1,0:T(8,128)(2,1)} %get-tuple-element.8), kind=kOutput, calls=%fused_computation | convolution fusion | flops 50724864 | bytes 1196032 | tf_op jit(solution)/shard_map/dot_general | solution.py:290

commit v2 on v1

v2 whole, which is shorter than its diff:
```python
import functools

import jax
import jax.numpy as jnp
from jax import lax
from jax.experimental import pallas as pl
from jax.experimental.pallas import tpu as pltpu
from jax.sharding import PartitionSpec as P

GATE_SCALE = 256.0
MESH = pl.DeviceIdType.MESH
F32 = jnp.float32
BF16 = jnp.bfloat16


def largest_tile(size, most):
    tile = most
    while size % tile:
        tile //= 2
    return tile


def kernel(nb, nd, cols_ch,
           tokens, ids, num, gate_w, up_w, down_w,
           slots_out, marks_out,
           x, packed, gw, uw, dw, accg, accu, away, back, hidden, term, got1, part, got2,
           loc_sem, own_send, own_recv, y_send, y_recv, fwd_send, fwd_recv,
           t_send, t_recv, s_send, s_recv,
           z_send, z_recv, x_send, x_recv, p1_send, p1_recv, p2_send, p2_recv):
    k = lax.axis_index("blk")
    j = lax.axis_index("dp")
    na, nc = nb // 2, nd // 2
    a, b = k // 2, k % 2
    y, core = j // 2, j % 2
    t_dev, depth = tokens.shape
    slots = t_dev // 2
    gate_rows, ff = gate_w.shape
    down_rows = down_w.shape[0]
    width = 2 * gate_rows
    nq = depth // cols_ch
    mate = (k, y * 2 + 1 - core)
    x_peer = (a * 2 + 1 - b, j)

    def y_dev(d):
        return (k, lax.rem(y + d, nc) * 2 + core)

    def z_chip(d):
        return lax.rem(a + d, na)

    def z_dev(d):
        return (z_chip(d) * 2 + b, j)

    def remote(src, dst, send, recv, device):
        return pltpu.make_async_remote_copy(
            src_ref=src, dst_ref=dst, send_sem=send, recv_sem=recv,
            device_id=device, device_id_type=MESH)

    def block(aa, bb):
        return bb * na + aa

    def block_rows(aa, bb):
        return pl.ds(pl.multiple_of(block(aa, bb) * slots, slots), slots)

    def piece(p, core_of, shard):
        if p < 2:
            rows = pl.ds(pl.multiple_of(core_of * gate_rows, 16), gate_rows)
            src, dst = ((gate_w, gw), (up_w, uw))[p]
            return src, dst.at[rows, :]
        q = p - 2
        return down_w.at[:, pl.ds(q * cols_ch, cols_ch)], dw.at[q, shard]

    pieces = 2 + nq

    peers = [mate, x_peer] + [y_dev(d) for d in range(1, nc)] + [z_dev(d) for d in range(1, na)]
    barrier = pltpu.get_barrier_semaphore()
    for peer in peers:
        pl.semaphore_signal(barrier, inc=1, device_id=peer, device_id_type=MESH)
    local = []
    for p in range(pieces):
        src, dst = piece(p, core, j)
        local.append(pltpu.make_async_copy(src, dst, loc_sem.at[p]))
        local[-1].start()

    hit0 = (ids[:, 0:1] == 0).astype(F32)
    hit1 = (ids[:, 1:2] == 0).astype(F32)
    hit = hit0 + hit1
    row = lax.broadcasted_iota(jnp.int32, (t_dev, t_dev), 0)
    col = lax.broadcasted_iota(jnp.int32, (t_dev, t_dev), 1)
    lower = (col <= row).astype(F32)
    place = jnp.dot(lower.astype(BF16), jnp.broadcast_to(hit, (t_dev, t_dev)).astype(BF16),
                    preferred_element_type=F32) - 1.0
    marks = jnp.where(place == col.astype(F32), 1.0, 0.0) * hit
    marks_out[...] = marks[:, :slots].astype(BF16)
    m0 = (marks * hit0).T[:slots]
    m1 = (marks * hit1).T[:slots]
    first = num[...].astype(F32) / GATE_SCALE
    weight = jnp.sum(m0 * first + m1 * (1.0 - first), axis=1, keepdims=True)
    packer = (m0 + m1).astype(BF16)

    def pack(d):
        columns = pl.ds(pl.multiple_of(lax.rem(y + d, nc) * width, 128), width)
        return jnp.dot(packer, tokens[:, columns], preferred_element_type=F32).astype(BF16)

    mine = block(a, b)
    for d in range(1, nc):
        packed[d - 1] = pack(d)
    x[mine, 0] = pack(0)

    pl.semaphore_wait(barrier, len(peers))

    copies = []

    def send(*args):
        copies.append(remote(*args))
        copies[-1].start()

    for d in range(1, nc):
        send(packed.at[d - 1], x.at[mine, nc - d], t_send.at[d - 1], t_recv.at[d - 1], y_dev(d))
    for p in range(2):
        src, dst = piece(p, core, j)
        send(src, dst, own_send.at[p], own_recv.at[p], mate)

    def send_down(q):
        src, dst = piece(2 + q, core, j)
        for d in range(1, nc):
            send(src, dst, y_send.at[d - 1, q], y_recv.at[d - 1, q], y_dev(d))

    early = min(1, nq)
    for q in range(early):
        send_down(q)
    send(x.at[mine, 0], x.at[mine, 0], x_send.at[0], x_recv.at[0], x_peer)
    for d in range(1, na):
        send(x.at[mine, 0], x.at[mine, 0], z_send.at[0, d - 1], z_recv.at[0, d - 1], z_dev(d))
    for d in range(1, nc):
        remote(packed.at[d - 1], x.at[mine, nc - d], t_send.at[d - 1], t_recv.at[d - 1], y_dev(d)).wait_recv()
    rest = x.at[mine, pl.ds(1, nc - 1)]
    send(rest, rest, x_send.at[na], x_recv.at[na], x_peer)
    for d in range(1, na):
        send(rest, rest, z_send.at[1, d - 1], z_recv.at[1, d - 1], z_dev(d))
    for p in range(2, pieces):
        src, dst = piece(p, core, j)
        send(src, dst, own_send.at[p], own_recv.at[p], mate)

    for p in range(2):
        local[p].wait()
        src, dst = piece(p, 1 - core, j)
        remote(src, dst, own_send.at[p], own_recv.at[p], mate).wait_recv()

    tile = largest_tile(ff, 256)

    def multiply_block(i, aa, bb):
        which = block(aa, bb)
        rows = block_rows(aa, bb)

        @pl.loop(0, ff // tile)
        def _(n):
            c0 = pl.multiple_of(n * tile, tile)
            cols = pl.ds(c0, tile)
            left = x[which].reshape(nc * slots, width)
            for w, acc, start in ((gw, accg, 0), (uw, accu, ff)):
                value = jnp.dot(left, w[:, cols], preferred_element_type=F32)
                acc[rows, cols] = value[:slots]
                for d in range(1, nc):
                    away[i, d - 1, :, pl.ds(pl.multiple_of(start + c0, tile), tile)] = (
                        value[d * slots:(d + 1) * slots].astype(BF16))

        for d in range(1, nc):
            send(away.at[i, d - 1], back.at[i, d - 1], s_send.at[i, d - 1], s_recv.at[i, d - 1], y_dev(d))

    def activate(i, aa, bb):
        rows = block_rows(aa, bb)
        for d in range(1, nc):
            remote(away.at[i, d - 1], back.at[i, d - 1], s_send.at[i, d - 1], s_recv.at[i, d - 1], y_dev(d)).wait_recv()

        @pl.loop(0, ff // tile)
        def _(n):
            c0 = pl.multiple_of(n * tile, tile)
            cols = pl.ds(c0, tile)
            g = accg[rows, cols]
            u = accu[rows, cols]
            for d in range(1, nc):
                g += back[i, d - 1, :, cols].astype(F32)
                u += back[i, d - 1, :, pl.ds(pl.multiple_of(ff + c0, tile), tile)].astype(F32)
            hidden[rows, cols] = (g / (1.0 + jnp.exp(-g)) * u).astype(BF16)

    order = []
    for d in range(na):
        source = lax.rem(a + na - d, na)
        order += [(source, b), (source, 1 - b)]
    lag = 2
    for i in range(nb + lag):
        if i < nb:
            d = i // 2
            aa, bb = order[i]
            here = x.at[block(aa, bb)]
            if i == 1:
                first_part = here.at[0]
                other_part = here.at[pl.ds(1, nc - 1)]
                remote(first_part, first_part, x_send.at[0], x_recv.at[0], x_peer).wait_recv()
                remote(other_part, other_part, x_send.at[na], x_recv.at[na], x_peer).wait_recv()
            elif i % 2:
                remote(here, here, x_send.at[d], x_recv.at[d], x_peer).wait_recv()
            elif i:
                first_part = here.at[0]
                other_part = here.at[pl.ds(1, nc - 1)]
                remote(first_part, first_part, z_send.at[0, d - 1], z_recv.at[0, d - 1], z_dev(d)).wait_recv()
                remote(other_part, other_part, z_send.at[1, d - 1], z_recv.at[1, d - 1], z_dev(d)).wait_recv()
                send(here, here, x_send.at[d], x_recv.at[d], x_peer)
            multiply_block(i, aa, bb)
            if i == nb - 1:
                for q in range(early, nq):
                    send_down(q)
        if i >= lag:
            activate(i - lag, *order[i - lag])

    rows_all = nb * slots
    half = na * slots
    mtile = largest_tile(rows_all, 256)

    def multiply(q):
        for d in range(1, nc):
            came = dw.at[q, lax.rem(y + nc - d, nc) * 2 + core]
            remote(came, came, y_send.at[d - 1, q], y_recv.at[d - 1, q], y_dev(d)).wait_recv()
            send(came, came, fwd_send.at[d - 1, q], fwd_recv.at[d - 1, q], mate)
        local[2 + q].wait()
        theirs = dw.at[q, y * 2 + 1 - core]
        remote(theirs, theirs, own_send.at[2 + q], own_recv.at[2 + q], mate).wait_recv()
        for d in range(1, nc):
            came = dw.at[q, lax.rem(y + nc - d, nc) * 2 + 1 - core]
            remote(came, came, fwd_send.at[d - 1, q], fwd_recv.at[d - 1, q], mate).wait_recv()

        @pl.loop(0, rows_all // mtile)
        def _(i):
            rows = pl.ds(pl.multiple_of(i * mtile, mtile), mtile)
            term[q, rows, :] = jnp.dot(
                hidden[rows, :], dw[q].reshape(nd * down_rows, cols_ch),
                preferred_element_type=F32).astype(BF16)

        other = pl.ds(pl.multiple_of((1 - b) * half, half), half)
        send(term.at[q, other, :], got1.at[q], p1_send.at[q], p1_recv.at[q], x_peer)

    def pair(q):
        remote(got1.at[q], got1.at[q], p1_send.at[q], p1_recv.at[q], x_peer).wait_recv()
        here = pl.ds(pl.multiple_of(b * half, half), half)
        part[q] = (term[q, here, :].astype(F32) + got1[q].astype(F32)).astype(BF16)
        for d in range(1, na):
            rows = pl.ds(pl.multiple_of(z_chip(d) * slots, slots), slots)
            send(part.at[q, rows, :], got2.at[q, d - 1],
                 p2_send.at[q, d - 1], p2_recv.at[q, d - 1], z_dev(d))

    def finish(q):
        for d in range(1, na):
            remote(got2.at[q, d - 1], got2.at[q, d - 1],
                   p2_send.at[q, d - 1], p2_recv.at[q, d - 1], z_dev(d)).wait_recv()
        total = part[q, pl.ds(pl.multiple_of(a * slots, slots), slots), :].astype(F32)
        for d in range(1, na):
            total += got2[q, d - 1].astype(F32)
        slots_out[:, pl.ds(q * cols_ch, cols_ch)] = (weight * total).astype(BF16)

    for q in range(nq + 2):
        if q < nq:
            multiply(q)
        if 1 <= q <= nq:
            pair(q - 1)
        if q >= 2:
            finish(q - 2)

    for copy in copies:
        copy.wait_send()


def on_device(nb, nd, tokens, expert_ids, gate_num, gate_weight, up_weight, down_weight):
    t_dev, depth = tokens.shape
    slots = t_dev // 2
    gate_rows, ff = gate_weight.shape
    down_rows = down_weight.shape[0]
    cols_ch = largest_tile(depth, 256)
    nq = depth // cols_ch
    pieces = 2 + nq
    na, nc = nb // 2, nd // 2
    rows_all = nb * slots
    dma = pltpu.SemaphoreType.DMA
    vmem = pl.BlockSpec(memory_space=pltpu.VMEM)
    hbm = pl.BlockSpec(memory_space=pl.ANY)
    far, deep = max(nc - 1, 1), max(na - 1, 1)
    packed, marks = pl.pallas_call(
        functools.partial(kernel, nb, nd, cols_ch),
        out_shape=(jax.ShapeDtypeStruct((slots, depth), BF16),
                   jax.ShapeDtypeStruct((t_dev, slots), BF16)),
        in_specs=[vmem, vmem, vmem, hbm, hbm, hbm],
        out_specs=(vmem, vmem),
        scratch_shapes=[
            pltpu.VMEM((nb, nc, slots, 2 * gate_rows), BF16),
            pltpu.VMEM((far, slots, 2 * gate_rows), BF16),
            pltpu.VMEM((2 * gate_rows, ff), BF16),
            pltpu.VMEM((2 * gate_rows, ff), BF16),
            pltpu.VMEM((nq, nd, down_rows, cols_ch), BF16),
            pltpu.VMEM((rows_all, ff), F32),
            pltpu.VMEM((rows_all, ff), F32),
            pltpu.VMEM((nb, far, slots, 2 * ff), BF16),
            pltpu.VMEM((nb, far, slots, 2 * ff), BF16),
            pltpu.VMEM((rows_all, ff), BF16),
            pltpu.VMEM((nq, rows_all, cols_ch), BF16),
            pltpu.VMEM((nq, na * slots, cols_ch), BF16),
            pltpu.VMEM((nq, na * slots, cols_ch), BF16),
            pltpu.VMEM((nq, deep, slots, cols_ch), BF16),
            dma((pieces,)), dma((pieces,)), dma((pieces,)),
            dma((far, nq)), dma((far, nq)), dma((far, nq)), dma((far, nq)),
            dma((far,)), dma((far,)), dma((nb, far)), dma((nb, far)),
            dma((2, deep)), dma((2, deep)), dma((na + 1,)), dma((na + 1,)),
            dma((nq,)), dma((nq,)), dma((nq, deep)), dma((nq, deep)),
        ],
        compiler_params=pltpu.CompilerParams(
            collective_id=0, has_side_effects=True, vmem_limit_bytes=67043328),
    )(tokens, expert_ids, gate_num.reshape(1, t_dev), gate_weight, up_weight, down_weight)
    return jnp.dot(marks, packed, preferred_element_type=F32).astype(BF16)


def solution(mesh):
    return jax.shard_map(
        functools.partial(on_device, mesh.shape["blk"], mesh.shape["dp"]),
        mesh=mesh,
        in_specs=(
            P(("blk", "dp"), None),
            P(("blk", "dp"), None),
            P(("blk", "dp")),
            P("dp", "blk"),
            P("dp", "blk"),
            P(("blk", "dp"), None),
        ),
        out_specs=P(("blk", "dp"), None),
        check_vma=False,
    )
```

time: 132 us -> 135 us (1.023)
  Pallas kernels: 128 us -> 131 us
    pallas_call x1, Pallas kernels: 128 us -> 131 us  [on_device(): pl.pallas_call(functools.partial(kernel, nb, nd, cols_ch), out_shape=(jax...]
where the time goes in v2:
time: 135 us
  Pallas kernels  131 us (97%)
  matrix products  2.25 us (2%)
  local copies, waits for them, and re-layouts  1.41 us (1%)
    pallas_call x1, Pallas kernels, on_device(): pl.pallas_call(functools.partial(kernel, nb, nd, cols_ch), out_shape=(jax...  131 us

profile of v2, /device:TPU:0, one launch (start us, length us, event | category | flops | bytes accessed | tf_op | source)
XLA Modules:
  0.0 134.7 jit_solution(1114198650843187213)
XLA Ops:
  0.0 1.4 %copy.7.ids = s32[128,2]{1,0:T(8,128)} copy(s32[128,2]{0,1:T(2,128)} %param.7) | data formatting | bytes 2048 | tf_op args[1]
  1.4 131.0 %shard_map.64 = (bf16[64,3072]{1,0:T(8,128)(2,1)}, bf16[128,64]{1,0:T(8,128)(2,1)}) custom-call(bf16[128,3072]{1,0:T(8,128)(2,1)} %tokens.1, s32[128,2]{1,0:T(8,128)} %copy.7.ids, s32[1,128]{1,0:T(1,128)} %bitcast.3, bf16[768,1024]{1,0:T(8,128)(2,1)} %gate_w.1, bf16[768,1024]{1,0:T(8,128)(2,1)} %up_w.1, bf16[256,3072]{1,0:T(8,128)(2,1)} %down_w.1), custom_call_target="tpu_custom_call" | custom-call | tf_op jit(solution)/shard_map/pallas_call | solution.py:286
  132.4 2.2 %convolution_convert_fusion = bf16[128,3072]{1,0:T(8,128)(2,1)} fusion(bf16[128,64]{1,0:T(8,128)(2,1)} %get-tuple-element.7, bf16[64,3072]{1,0:T(8,128)(2,1)} %get-tuple-element.8), kind=kOutput, calls=%fused_computation | convolution fusion | flops 50724864 | bytes 1196032 | tf_op jit(solution)/shard_map/dot_general | solution.py:316

commit v3 on v1

--- a/solution.py
+++ b/solution.py
@@ -252,7 +252,7 @@
     rows_ch = largest_tile(gate_rows, 256)
     if rows_ch % 128:
         rows_ch = gate_rows
-    cols_ch = largest_tile(depth, 512)
+    cols_ch = largest_tile(depth, 256)
     n_ch, nq = gate_rows // rows_ch, depth // cols_ch
     pieces = 2 * n_ch + nq
     na, nc = nb // 2, nd // 2

time: 132 us -> 138 us (1.045)
  Pallas kernels: 128 us -> 134 us
    pallas_call x1, Pallas kernels: 128 us -> 134 us  [on_device(): pl.pallas_call(functools.partial(kernel, nb, nd, rows_ch, cols_ch), out_s...]
where the time goes in v3:
time: 138 us
  Pallas kernels  134 us (97%)
  matrix products  2.24 us (2%)
  local copies, waits for them, and re-layouts  1.41 us (1%)
    pallas_call x1, Pallas kernels, on_device(): pl.pallas_call(functools.partial(kernel, nb, nd, rows_ch, cols_ch), out_s...  134 us

profile of v3, /device:TPU:0, one launch (start us, length us, event | category | flops | bytes accessed | tf_op | source)
XLA Modules:
  0.0 138.1 jit_solution(5077780110618879123)
XLA Ops:
  0.0 1.4 %copy.7.ids = s32[128,2]{1,0:T(8,128)} copy(s32[128,2]{0,1:T(2,128)} %param.7) | data formatting | bytes 2048 | tf_op args[1]
  1.4 134.4 %shard_map.64 = (bf16[64,3072]{1,0:T(8,128)(2,1)}, bf16[128,64]{1,0:T(8,128)(2,1)}) custom-call(bf16[128,3072]{1,0:T(8,128)(2,1)} %tokens.1, s32[128,2]{1,0:T(8,128)} %copy.7.ids, s32[1,128]{1,0:T(1,128)} %bitcast.3, bf16[768,1024]{1,0:T(8,128)(2,1)} %gate_w.1, bf16[768,1024]{1,0:T(8,128)(2,1)} %up_w.1, bf16[256,3072]{1,0:T(8,128)(2,1)} %down_w.1), custom_call_target="tpu_custom_call" | custom-call | tf_op jit(solution)/shard_map/pallas_call | solution.py:264
  135.9 2.2 %convolution_convert_fusion = bf16[128,3072]{1,0:T(8,128)(2,1)} fusion(bf16[128,64]{1,0:T(8,128)(2,1)} %get-tuple-element.7, bf16[64,3072]{1,0:T(8,128)(2,1)} %get-tuple-element.8), kind=kOutput, calls=%fused_computation | convolution fusion | flops 50724864 | bytes 1196032 | tf_op jit(solution)/shard_map/dot_general | solution.py:290
